TPU v7x, 32 devices: a whole 2x2x4 slice. The times are simulated.
32 devices in a mesh: dp: 2 (over x), ctx: 16 (over z, y, core).
Axes of the slice: x: 2, y: 2, z: 4, core: 2. Of those that a mesh axis runs over, the one named last changes fastest.
Arguments:
- patches: bfloat16 [2, 1024, 1280], P('dp', 'ctx'), may hold values from -6 to 6
- vit_norm_gain: float32 [1280], replicated, may hold values from 0.1 to 1.9
- vit_qkv: bfloat16 [1280, 1920], P('dp'), may hold values from -0.15625 to 0.15625
- vit_out: bfloat16 [640, 1280], P('dp'), may hold values from -0.25 to 0.25
- merger: bfloat16 [5120, 8192], P('dp', 'ctx'), may hold values from -0.078125 to 0.078125
- text_embed: bfloat16 [2, 2048, 8192], P('dp', 'ctx'), may hold values from -6 to 6
- lang_norm_gain: float32 [8192], replicated, may hold values from 0.1 to 1.9
- key_weight: bfloat16 [8192, 512], P('dp'), may hold values from -0.0625 to 0.0625
- key_cotangent: bfloat16 [2, 2048, 512], P('dp', 'ctx'), may hold values from -6 to 6
- image_grid: int32 [2, 16, 2], P('dp'), may hold values from 1 to 16, as said below
- image_start: int32 [2, 16], P('dp'), may hold values from 0 to 2047, as said below
Outputs:
- key_rot: bfloat16 [2, 2048, 512], P('dp', 'ctx')
- merger_grad: float32 [5120, 8192], P('dp', 'ctx')
Inputs may be any that keep to these rules, and one draw needn't show every extreme that they name: `image_grid`: the image held by device c of ctx has a grid of rows by columns merged tokens with rows times columns at most 16, equal to 16 for some device of every sequence. Its 4 * rows * columns patches are the first rows of that device's patch block, each 2x2 merge window as 4 consecutive rows, windows in row-major order; the remaining rows are unused. `image_start`: the image occupies rows * columns consecutive positions from here. The range of 128 positions of each device along ctx holds exactly one image, wholly.
All inputs are finite; a program needn't handle non-finite values.
Results may differ from a plain program's by a relative error of at most 0.015.
Values may be sent and summed in bfloat16 or wider, within the bound.
No kernel may reach another device: no remote copies, remote signals or barrier semaphores. Data moves between devices by JAX's collectives and lax.ppermute only.
A program may use at most 128 MiB of HBM per device.

v0:
```python
import math
import jax
import jax.numpy as jnp
from jax import lax
from jax.sharding import PartitionSpec as P

VHD = 80
HD = 128
EPS = 1e-06
THETA = 1000000.0


def layer_norm(values):
    average = jnp.mean(values, axis=-1, keepdims=True)
    centered = values - average
    variance = jnp.mean(centered * centered, axis=-1, keepdims=True)
    return centered * lax.rsqrt(variance + EPS)


def vision_image(patch_rows, count, norm_gain, qkv_weight, out_weight):
    values = patch_rows.astype(jnp.float32)
    normed = (layer_norm(values) * norm_gain).astype(jnp.bfloat16)
    projected = jnp.dot(normed, qkv_weight, preferred_element_type=jnp.float32).astype(jnp.bfloat16)
    width = qkv_weight.shape[1] // 3
    head_count = width // VHD
    queries = projected[:, :width].reshape(-1, head_count, VHD)
    key_vecs = projected[:, width : 2 * width].reshape(-1, head_count, VHD)
    value_vecs = projected[:, 2 * width :].reshape(-1, head_count, VHD)
    scores = jnp.einsum(
        "qhd,khd->hqk", queries, key_vecs, preferred_element_type=jnp.float32
    ) / math.sqrt(VHD)
    alive_mask = (jnp.arange(values.shape[0], dtype=jnp.int32) < 4 * count).astype(jnp.float32)
    weights = jnp.exp(scores) * alive_mask[None, None, :]
    probability = (weights / jnp.sum(weights, axis=-1, keepdims=True)).astype(jnp.bfloat16)
    attended = jnp.einsum(
        "hqk,khd->qhd", probability, value_vecs, preferred_element_type=jnp.float32
    )
    attended = attended.reshape(values.shape[0], width).astype(jnp.bfloat16)
    vit_hidden = values + jnp.dot(attended, out_weight, preferred_element_type=jnp.float32)
    merged = layer_norm(vit_hidden).astype(jnp.bfloat16).reshape(-1, 4 * values.shape[1])
    keeping = jnp.arange(merged.shape[0], dtype=jnp.int32) < count
    return jnp.where(keeping[:, None], merged, jnp.zeros_like(merged))


def rope_tables(pos_t, pos_h, pos_w):
    half_dim = HD // 2
    freq_index = jnp.arange(half_dim, dtype=jnp.int32)
    inverse = THETA ** (-(2.0 * freq_index.astype(jnp.float32)) / HD)
    first_cut = HD // 8
    second_cut = first_cut + 3 * HD // 16
    chosen = jnp.where(
        freq_index[None, :] < first_cut,
        pos_t[:, None],
        jnp.where(freq_index[None, :] < second_cut, pos_h[:, None], pos_w[:, None]),
    )
    angles = chosen.astype(jnp.float32) * inverse[None, :]
    return (jnp.cos(angles), jnp.sin(angles))


def rotate(vectors, cosine, sines):
    half_dim = vectors.shape[-1] // 2
    first_half = vectors[..., :half_dim]
    second_half = vectors[..., half_dim:]
    cos_part = cosine[:, None, :]
    sin_part = sines[:, None, :]
    return jnp.concatenate(
        [
            first_half * cos_part - second_half * sin_part,
            second_half * cos_part + first_half * sin_part,
        ],
        axis=-1,
    )


def unrotate(vectors, cosine, sines):
    half_dim = vectors.shape[-1] // 2
    first_half = vectors[..., :half_dim]
    second_half = vectors[..., half_dim:]
    cos_part = cosine[:, None, :]
    sin_part = sines[:, None, :]
    return jnp.concatenate(
        [
            first_half * cos_part + second_half * sin_part,
            second_half * cos_part - first_half * sin_part,
        ],
        axis=-1,
    )


def norm_backward(rows, grad_rows, gain):
    values = rows.astype(jnp.float32)
    row_scale = lax.rsqrt(jnp.mean(values * values, axis=-1, keepdims=True) + EPS)
    weighted = grad_rows * gain
    return row_scale * weighted - values * row_scale**3 * jnp.mean(
        values * weighted, axis=-1, keepdims=True
    )


def on_device(
    patches,
    vit_norm_gain,
    vit_qkv,
    vit_out,
    merger,
    text_embed,
    lang_norm_gain,
    key_weight,
    key_cotangent,
    image_grid,
    image_start,
):
    tokens = text_embed.shape[1]
    groups = lax.axis_size("ctx")
    own_index = lax.axis_index("ctx")
    qkv_full, out_full, merger_rows = (
        lax.all_gather(vit_qkv, "dp", axis=0, tiled=True),
        lax.all_gather(vit_out, "dp", axis=0, tiled=True),
        lax.all_gather(merger, "dp", axis=0, tiled=True),
    )
    grid_sizes = image_grid[0]
    start_pos = image_start[0]
    grid_rows = grid_sizes[:, 0]
    grid_cols = grid_sizes[:, 1]
    counts = grid_rows * grid_cols
    own_count = lax.dynamic_index_in_dim(counts, own_index, 0, keepdims=False)
    merged = vision_image(patches[0], own_count, vit_norm_gain, qkv_full, out_full)
    capacity = merged.shape[0]
    merged_all = lax.all_gather(merged, "ctx", axis=0, tiled=True)
    embedded = jnp.dot(merged_all, merger_rows, preferred_element_type=jnp.float32).astype(
        jnp.bfloat16
    )
    blocks = embedded.reshape(groups, capacity, -1)
    target_range = start_pos // tokens
    routing = (target_range[None, :] == jnp.arange(groups, dtype=jnp.int32)[:, None]).astype(
        jnp.bfloat16
    )
    outgoing = jnp.einsum(
        "do,okc->dkc", routing, blocks, preferred_element_type=jnp.float32
    ).astype(jnp.bfloat16)
    arrived = lax.all_to_all(outgoing, "ctx", split_axis=0, concat_axis=2, tiled=True)[0]
    own_range = target_range == own_index
    image_first = jnp.sum(jnp.where(own_range, start_pos, 0))
    own_cols = jnp.sum(jnp.where(own_range, grid_cols, 0))
    image_count = jnp.sum(jnp.where(own_range, counts, 0))
    offset = image_first - own_index * tokens
    local_index = jnp.arange(tokens, dtype=jnp.int32)
    inner_index = local_index - offset
    image_mask = (inner_index >= 0) & (inner_index < image_count)
    slot_index = jnp.arange(capacity, dtype=jnp.int32)
    slot_alive = slot_index < image_count
    selector = (inner_index[:, None] == slot_index[None, :]) & slot_alive[None, :]
    placed = jnp.dot(
        selector.astype(jnp.bfloat16), arrived, preferred_element_type=jnp.float32
    ).astype(jnp.bfloat16)
    hidden = jnp.where(image_mask[:, None], placed, text_embed[0])
    hidden_float = hidden.astype(jnp.float32)
    row_scale = lax.rsqrt(jnp.mean(hidden_float * hidden_float, axis=-1, keepdims=True) + EPS)
    normed = (hidden_float * row_scale * lang_norm_gain).astype(jnp.bfloat16)
    pieces = lax.all_to_all(normed, "dp", split_axis=1, concat_axis=0, tiled=True)
    key_proj = lax.psum_scatter(
        jnp.dot(pieces, key_weight, preferred_element_type=jnp.float32).astype(jnp.bfloat16),
        "dp",
        scatter_dimension=0,
        tiled=True,
    ).astype(jnp.float32)
    global_index = own_index * tokens + local_index
    inner_safe = jnp.clip(inner_index, 0, capacity - 1)
    pos_t = jnp.where(image_mask, image_first, global_index)
    pos_h = jnp.where(image_mask, image_first + inner_safe // own_cols, global_index)
    pos_w = jnp.where(image_mask, image_first + inner_safe % own_cols, global_index)
    cosine, sines = rope_tables(pos_t, pos_h, pos_w)
    head_count = key_weight.shape[1] // HD
    rotated = (
        rotate(key_proj.reshape(tokens, head_count, HD), cosine, sines)
        .reshape(tokens, -1)
        .astype(jnp.bfloat16)
    )
    grad_key = unrotate(
        key_cotangent[0].astype(jnp.float32).reshape(tokens, head_count, HD), cosine, sines
    ).reshape(tokens, -1)
    grad_image_key = jnp.dot(
        selector.T.astype(jnp.float32), grad_key, precision=lax.Precision.HIGHEST
    ).astype(jnp.bfloat16)
    all_grads = lax.all_gather(grad_image_key, "dp", axis=0, tiled=True)
    partial_value = lax.dot_general(
        all_grads, key_weight, (((1,), (1,)), ((), ())), preferred_element_type=jnp.float32
    )
    grad_normed = lax.all_to_all(
        partial_value.astype(jnp.bfloat16), "dp", split_axis=0, concat_axis=1, tiled=True
    ).astype(partial_value.dtype)
    grad_hidden = norm_backward(arrived, grad_normed, lang_norm_gain)
    grad_embedded = jnp.where(slot_alive[:, None], grad_hidden, 0.0).astype(jnp.bfloat16)
    returned = lax.all_to_all(grad_embedded[None], "ctx", split_axis=2, concat_axis=0, tiled=True)
    grad_blocks = jnp.einsum(
        "do,dkc->okc", routing, returned, preferred_element_type=jnp.float32
    ).astype(jnp.bfloat16)
    grad_all = grad_blocks.reshape(groups * capacity, -1)
    merger_grad = lax.psum_scatter(
        lax.dot_general(
            merged_all, grad_all, (((0,), (0,)), ((), ())), preferred_element_type=jnp.float32
        ).astype(jnp.bfloat16),
        "dp",
        scatter_dimension=0,
        tiled=True,
    ).astype(jnp.float32)
    return (rotated[None], merger_grad)


def solution(mesh):
    return jax.shard_map(
        on_device,
        mesh=mesh,
        in_specs=(
            P("dp", "ctx", None),
            P(),
            P("dp", None),
            P("dp", None),
            P("dp", "ctx"),
            P("dp", "ctx", None),
            P(),
            P("dp", None),
            P("dp", "ctx", None),
            P("dp", None, None),
            P("dp", None),
        ),
        out_specs=(P("dp", "ctx", None), P("dp", "ctx")),
        check_vma=False,
    )
```

profile of v0, /device:TPU:0, one launch (start us, length us, event | category | flops | bytes accessed | tf_op | source)
XLA Modules:
  0.0 469.2 jit_solution(12247656343845873802)
XLA Ops:
  7.2 0.7 all-gather.5.cloned.1.call-update
  8.0 0.7 all-gather.7.cloned.1.call-update
  8.7 0.7 all-gather.11.cloned.1.call-update
  9.5 0.7 fusion.37
  10.2 0.6 dynamic_slice.4
  11.4 0.7 iota_compare_fusion.4
  12.5 64.7 %all-gather.5.cloned.1.call-done = bf16[1280,1920]{1,0:T(8,128)(2,1)} async-done(((bf16[640,1920]{1,0:T(8,128)(2,1)}), bf16[1280,1920]{1,0:T(8,128)(2,1)}) %all-gather.5.cloned.1.call-update) | async-done | bytes 4915216 | tf_op jit(solution)/shard_map/all_gather | solution.py:116
  77.2 3.4 convolution_convert_fusion.3
  81.8 24.8 %all-gather.7.cloned.1.call-done = bf16[640,1280]{1,0:T(8,128)(2,1)} async-done(((bf16[320,1280]{1,0:T(8,128)(2,1)}), bf16[640,1280]{1,0:T(8,128)(2,1)}) %all-gather.7.cloned.1.call-update) | async-done | bytes 1638416 | tf_op jit(solution)/shard_map/all_gather | solution.py:117
  106.7 1.9 fusion.49
  109.0 0.8 broadcast_select_fusion
  109.8 67.0 %all-gather.11.cloned.1.call-done = bf16[5120,512]{1,0:T(8,128)(2,1)} async-done(((bf16[2560,512]{1,0:T(8,128)(2,1)}), bf16[5120,512]{1,0:T(8,128)(2,1)}) %all-gather.11.cloned.1.call-update) | async-done | bytes 5242896 | tf_op jit(solution)/shard_map/all_gather | solution.py:118
  176.8 45.8 %all-gather.9.cloned.1.call-done = bf16[256,5120]{1,0:T(8,128)(2,1)} async-done(((bf16[16,5120]{1,0:T(8,128)(2,1)}), bf16[256,5120]{1,0:T(8,128)(2,1)}) %all-gather.9.cloned.1.call-update) | async-done | bytes 2621456 | tf_op jit(solution)/shard_map/all_gather | solution.py:128
  222.6 4.8 %convolution_convert_fusion.7 = bf16[256,512]{1,0:T(8,128)(2,1)S(1)} fusion(bf16[256,5120]{1,0:T(8,128)(2,1)} %all-gather.9.cloned.1.call-done, bf16[5120,512]{1,0:T(8,128)(2,1)} %all-gather.11.cloned.1.call-done), kind=kOutput, calls=%fused_computation.13 | convolution fusion | flops 1342308352 | bytes 8126464 | tf_op jit(solution)/shard_map/dot_general | solution.py:129
  227.4 0.4 convolution_convert_fusion.6
  227.8 0.9 copy.48
  228.6 3.6 all-to-all-start
  234.8 0.6 iota_compare_fusion.5
  235.4 1.3 fusion.39
  236.7 1.4 add_select_fusion.1
  238.1 4.0 all-to-all-done
  242.2 0.9 multiply_reduce_fusion
  243.1 0.5 multiply_convert_fusion
  243.8 28.0 %all_to_all.65 = bf16[128,2,4096]{2,0,1:T(8,128)(2,1)S(1)} all-to-all(bf16[128,2,4096]{2,0,1:T(8,128)(2,1)S(1)} %bitcast.113), channel_id=1, replica_groups=mesh['dp'=2,'ctx'=16] {'dp'}, dimensions={1} | all-to-all | bytes 4194304 | tf_op jit(solution)/shard_map/all_to_all | solution.py:159
  271.8 2.0 convolution_convert_fusion.5
  274.0 0.3 fusion.24
  274.3 9.1 %reduce-scatter.3.cloned.1.call-done = bf16[128,512]{1,0:T(8,128)(2,1)} async-done(((bf16[256,512]{1,0:T(8,128)(2,1)}), bf16[128,512]{1,0:T(8,128)(2,1)}) %reduce-scatter.3.cloned.1.call-update) | async-done | bytes 131088 | tf_op jit(solution)/shard_map/reduce_scatter | solution.py:160
  283.4 1.0 reshape.495
  284.4 0.5 multiply_add_fusion
  285.3 4.4 all_gather.19
  289.7 4.2 convolution_convert_fusion.2
  294.0 3.4 all-to-all-start.2
  297.9 4.7 all-to-all-done.2
  302.6 0.4 copy.51
  303.0 0.5 reshape.499
  303.5 0.5 reshape.497
  303.9 0.3 multiply_reduce_fusion.2
  304.4 6.7 %copy.53 = bf16[1,16,8192]{1,0,2:T(2,128)(2,1)} copy(bf16[1,16,8192]{2,1,0:T(8,128)(2,1)S(1)} %select_convert_fusion) | data formatting | bytes 524288 | tf_op jit(solution)/shard_map/convert_element_type | solution.py:192
  311.1 0.5 broadcast.478
  311.6 45.2 %reduce.3 = bf16[8192,16]{1,0:T(8,128)(2,1)S(1)} reduce(bf16[8192,1,16]{2,1,0:T(2,128)(2,1)} %bitcast.110, bf16[]{:T(256)} %broadcast.478), dimensions={1}, to_apply=%bitcast.90.reduce_sub_computation | reduce | bytes 524290
  356.8 2.1 reshape.502
  359.0 15.4 %all_to_all.66 = bf16[16,2,4096]{2,1,0:T(2,128)(2,1)S(1)} all-to-all(bf16[16,2,4096]{2,1,0:T(2,128)(2,1)S(1)} %reshape.502), channel_id=1, replica_groups=mesh['dp'=2,'ctx'=16] {'ctx'}, dimensions={0} | all-to-all | bytes 524288 | tf_op jit(solution)/shard_map/all_to_all | solution.py:193
  374.4 7.6 %reshape.503 = bf16[8192,1,16]{2,1,0:T(2,128)(2,1)} reshape(bf16[16,2,4096]{2,1,0:T(2,128)(2,1)S(1)} %all_to_all.66) | data formatting | bytes 524288
  382.0 7.9 %copy.54 = bf16[1,16,8192]{2,1,0:T(8,128)(2,1)S(1)} copy(bf16[1,16,8192]{1,0,2:T(2,128)(2,1)} %bitcast.111) | data formatting | bytes 524288 | tf_op jit(solution)/shard_map/all_to_all | solution.py:193
  390.4 3.9 convolution_convert_fusion.1
  394.6 0.7 convert_element_type.180
  395.3 62.3 %reduce-scatter.5.cloned.1.call-done = bf16[2560,512]{1,0:T(8,128)(2,1)} async-done(((bf16[5120,512]{1,0:T(8,128)(2,1)}), bf16[2560,512]{1,0:T(8,128)(2,1)}) %reduce-scatter.5.cloned.1.call-update) | async-done | bytes 2621456 | tf_op jit(solution)/shard_map/reduce_scatter | solution.py:198
  457.6 4.8 %convert_element_type.196 = f32[2560,512]{1,0:T(8,128)} convert(bf16[2560,512]{1,0:T(8,128)(2,1)} %reduce-scatter.5.cloned.1.call-done) | non-fusion elementwise | flops 1310720 | bytes 7864320 | tf_op jit(solution)/shard_map/convert_element_type | solution.py:205
  (65 shorter events, 4.4 us)
Async XLA Ops:
  7.2 2.3 copy-start.7
  7.2 2.3 copy-start.8
  7.2 4.9 %copy-start.2 = (bf16[1,64,1280]{2,1,0:T(8,128)(2,1)S(1)}, bf16[1,64,1280]{2,1,0:T(8,128)(2,1)}, u32[]{:S(2)}) copy-start(bf16[1,64,1280]{2,1,0:T(8,128)(2,1)} %param.11) | copy-start | bytes 491524
  7.2 70.0 %copy-start.6 = (f32[1280]{0:T(1024)S(1)}, f32[1280]{0:T(1024)}, u32[]{:S(2)}) copy-start(f32[1280]{0:T(1024)} %param.12) | copy-start | bytes 15364
  7.2 70.0 %all-gather.5.cloned.1.call-start = ((), (), s32[]{:S(2)}) async-start(), calls=%async_computation.6 | async-start | bytes 7372800 | tf_op jit(solution)/shard_map/all_gather | solution.py:116
  7.9 98.7 %all-gather.7.cloned.1.call-start = ((), (), s32[]{:S(2)}) async-start(), calls=%async_computation.7 | async-start | bytes 2457600 | tf_op jit(solution)/shard_map/all_gather | solution.py:117
  8.7 168.1 %all-gather.11.cloned.1.call-start = ((), (), s32[]{:S(2)}) async-start(), calls=%async_computation.9 | async-start | bytes 7864320 | tf_op jit(solution)/shard_map/all_gather | solution.py:118
  9.4 213.2 %all-gather.9.cloned.1.call-start = ((), (), s32[]{:S(2)}) async-start(), calls=%async_computation.8 | async-start | bytes 2785280 | tf_op jit(solution)/shard_map/all_gather | solution.py:128
  109.8 132.4 %copy-start.3 = (bf16[1,128,8192]{2,1,0:T(8,128)(2,1)S(1)}, bf16[1,128,8192]{2,1,0:T(8,128)(2,1)}, u32[]{:S(2)}) copy-start(bf16[1,128,8192]{2,1,0:T(8,128)(2,1)} %param.16) | copy-start | bytes 6291460
  227.7 15.4 %copy-start.4 = (f32[8192]{0:T(1024)S(1)}, f32[8192]{0:T(1024)}, u32[]{:S(2)}) copy-start(f32[8192]{0:T(1024)} %param.17) | copy-start | bytes 98308
  228.6 13.6 %all-to-all-start = ((bf16[16,16,512]{2,1,0:T(8,128)(2,1)}), bf16[16,16,512]{2,1,0:T(8,128)(2,1)S(1)}, u32[]{:S(2)}, u32[]{:S(2)}) async-start(bf16[16,16,512]{2,1,0:T(8,128)(2,1)} %copy.48), calls=%async_computation | async-start | bytes 524288 | tf_op jit(solution)/shard_map/all_to_all | solution.py:140
  232.2 51.2 %reduce-scatter.3.cloned.1.call-start = ((), (), s32[]{:S(2)}) async-start(), calls=%async_computation.10 | async-start | bytes 393216 | tf_op jit(solution)/shard_map/reduce_scatter | solution.py:160
  243.6 28.2 %copy-start.1 = (bf16[4096,512]{1,0:T(8,128)(2,1)S(1)}, bf16[4096,512]{1,0:T(8,128)(2,1)}, u32[]{:S(2)}) copy-start(bf16[4096,512]{1,0:T(8,128)(2,1)} %param.18) | copy-start | bytes 12582916
  271.8 2.1 copy-start.5
  294.0 8.6 %all-to-all-start.2 = ((bf16[2,16,4096]{2,1,0:T(8,128)(2,1)}), bf16[2,16,4096]{2,1,0:T(8,128)(2,1)S(1)}, u32[]{:S(2)}, u32[]{:S(2)}) async-start(bf16[2,16,4096]{2,1,0:T(8,128)(2,1)} %bitcast.17), calls=%async_computation.3 | async-start | bytes 524288 | tf_op jit(solution)/shard_map/all_to_all | solution.py:188
  297.4 160.2 %reduce-scatter.5.cloned.1.call-start = ((), (), s32[]{:S(2)}) async-start(), calls=%async_computation.11 | async-start | bytes 7864320 | tf_op jit(solution)/shard_map/reduce_scatter | solution.py:198
  374.4 16.0 %copy-start = (bf16[256,5120]{1,0:T(8,128)(2,1)S(1)}, bf16[256,5120]{1,0:T(8,128)(2,1)}, u32[]{:S(2)}) copy-start(bf16[256,5120]{1,0:T(8,128)(2,1)} %all-gather.9.cloned.1.call-done) | copy-start | bytes 7864324
Sparse Core Ops, SparseCore 0:
  9.6 67.5 all-gather.4
  78.7 27.9 all-gather.6
  108.2 68.5 all-gather.10
  179.5 43.0 all-gather.8
  274.0 9.3 reduce-scatter.2
  394.5 63.0 reduce-scatter.4
where the time goes:
time: 470 us; the launch traced here: 469 us
  waiting for transfers between devices  284 us (60%)
  other arithmetic  58.6 us (12%)
  blocking collectives  47.8 us (10%)
  local copies, waits for them, and re-layouts  30.7 us (7%)
  matrix products  22.5 us (5%)
  between operations  17.8 us (4%)
  starting transfers between devices  7.42 us (2%)
    all_gather x1, waiting for transfers between devices, on_device(): lax.all_gather(merger, 'dp', axis=0, tiled=True)  67 us
    all_gather x1, waiting for transfers between devices, on_device(): lax.all_gather(vit_qkv, 'dp', axis=0, tiled=True)  64.7 us
    reduce_scatter x1, waiting for transfers between devices, on_device(): lax.psum_scatter(lax.dot_general(merged_all, grad_all, (((0,), (0,)), (()...  62.3 us
    all_gather x1, waiting for transfers between devices, on_device(): merged_all = lax.all_gather(merged, 'ctx', axis=0, tiled=True)  45.8 us
    unnamed x1, other arithmetic  45.2 us
    all_to_all x1, blocking collectives, on_device(): lax.all_to_all(normed, 'dp', split_axis=1, concat_axis=0, tiled=True)  28 us
    all_gather x1, waiting for transfers between devices, on_device(): lax.all_gather(vit_out, 'dp', axis=0, tiled=True)  24.8 us
    all_to_all x1, blocking collectives, on_device(): lax.all_to_all(grad_embedded[None], 'ctx', split_axis=2, concat_axis=0, t...  15.4 us
  transfers between devices with their start and end apart: 8, of which 8 were waited for; matrix products, arithmetic and copies ran while one was open for 3% of the time, Pallas kernels for 0%

commit v1 on v0

--- a/solution.py
+++ b/solution.py
@@ -8,6 +8,17 @@
 HD = 128
 EPS = 1e-06
 THETA = 1000000.0
+
+
+def around_the_ring(x, axis, dim):
+    devices = lax.axis_size(axis)
+    route = [(i, (i + 1) % devices) for i in range(devices)]
+    parts = [x]
+    for far in range(1, devices):
+        parts = [lax.ppermute(parts[0], axis, route), *parts]
+    result = jnp.concatenate(parts, axis=dim)
+    shift = (lax.axis_index(axis) + 1) * parts[-1].shape[dim]
+    return jnp.roll(result, shift, axis=dim)
 
 
 def layer_norm(values):
@@ -125,7 +136,7 @@
     own_count = lax.dynamic_index_in_dim(counts, own_index, 0, keepdims=False)
     merged = vision_image(patches[0], own_count, vit_norm_gain, qkv_full, out_full)
     capacity = merged.shape[0]
-    merged_all = lax.all_gather(merged, "ctx", axis=0, tiled=True)
+    merged_all = around_the_ring(merged, "ctx", 0)
     embedded = jnp.dot(merged_all, merger_rows, preferred_element_type=jnp.float32).astype(
         jnp.bfloat16
     )

time: 470 us -> 526 us (1.12)
  waiting for transfers between devices: 284 us -> 313 us
  local copies, waits for them, and re-layouts: 30.7 us -> 51 us
    ppermute x0 -> x15, waiting for transfers between devices: none -> 112 us  [around_the_ring(): parts = [lax.ppermute(parts[0], axis, route), *parts]]
    all_gather x1 -> x0, waiting for transfers between devices: 45.8 us -> none  [on_device(): merged_all = lax.all_gather(merged, 'ctx', axis=0, tiled=True)]
    all_gather x1, waiting for transfers between devices: 67 us -> 32.2 us  [on_device(): lax.all_gather(merger, 'dp', axis=0, tiled=True)]
    unnamed x23 -> x47, local copies, waits for them, and re-layouts: 10.4 us -> 30.7 us
    unnamed x1 -> x2, other arithmetic: 45.2 us -> 46 us
  transfers between devices with their start and end apart: 8 -> 22, of which waited for: 8 -> 22; matrix products, arithmetic and copies ran while one was open for 3% -> 7% of each run, Pallas kernels for 0% -> 0%
where the time goes in v1:
time: 526 us; the launch traced here: 525 us
  waiting for transfers between devices  313 us (60%)
  other arithmetic  62.1 us (12%)
  local copies, waits for them, and re-layouts  51 us (10%)
  blocking collectives  47.8 us (9%)
  matrix products  24.3 us (5%)
  between operations  17.5 us (3%)
  starting transfers between devices  9.53 us (2%)
    ppermute x15, waiting for transfers between devices, around_the_ring(): parts = [lax.ppermute(parts[0], axis, route), *parts]  112 us
    all_gather x1, waiting for transfers between devices, on_device(): lax.all_gather(vit_qkv, 'dp', axis=0, tiled=True)  62.8 us
    reduce_scatter x1, waiting for transfers between devices, on_device(): lax.psum_scatter(lax.dot_general(merged_all, grad_all, (((0,), (0,)), (()...  62.3 us
    unnamed x2, other arithmetic  46 us
    all_gather x1, waiting for transfers between devices, on_device(): lax.all_gather(merger, 'dp', axis=0, tiled=True)  32.2 us
    unnamed x47, local copies, waits for them, and re-layouts  30.7 us
    all_to_all x1, blocking collectives, on_device(): lax.all_to_all(normed, 'dp', split_axis=1, concat_axis=0, tiled=True)  28 us
    all_gather x1, waiting for transfers between devices, on_device(): lax.all_gather(vit_out, 'dp', axis=0, tiled=True)  24.7 us
  transfers between devices with their start and end apart: 22, of which 22 were waited for; matrix products, arithmetic and copies ran while one was open for 7% of the time, Pallas kernels for 0%

profile of v1, /device:TPU:0, one launch (start us, length us, event | category | flops | bytes accessed | tf_op | source)
XLA Modules:
  0.0 524.9 jit_solution(5358705703779297928)
XLA Ops:
  8.7 1.5 fusion.43
  12.1 1.0 convert_reduce_fusion
  13.2 1.1 fusion.14
  14.3 62.8 %all-gather.4.cloned.1.call-done = bf16[1280,1920]{1,0:T(8,128)(2,1)} async-done(((bf16[640,1920]{1,0:T(8,128)(2,1)}), bf16[1280,1920]{1,0:T(8,128)(2,1)}) %all-gather.4.cloned.1.call-update) | async-done | bytes 4915216 | tf_op jit(solution)/shard_map/all_gather | solution.py:127
  77.1 3.5 convolution_convert_fusion.3
  81.9 24.7 %all-gather.6.cloned.1.call-done = bf16[640,1280]{1,0:T(8,128)(2,1)} async-done(((bf16[320,1280]{1,0:T(8,128)(2,1)}), bf16[640,1280]{1,0:T(8,128)(2,1)}) %all-gather.6.cloned.1.call-update) | async-done | bytes 1638416 | tf_op jit(solution)/shard_map/all_gather | solution.py:128
  106.6 1.9 fusion.57
  109.1 7.4 %collective-permute-done = bf16[16,5120]{1,0:T(8,128)(2,1)S(1)} collective-permute-done((bf16[16,5120]{1,0:T(8,128)(2,1)S(1)}, bf16[16,5120]{1,0:T(8,128)(2,1)S(1)}, u32[]{:S(2)}, u32[]{:S(2)}) %collective-permute-start) | collective-permute-done | bytes 163872 | tf_op jit(solution)/shard_map/ppermute | solution.py:18
  116.6 7.4 %collective-permute-done.1 = bf16[16,5120]{1,0:T(8,128)(2,1)S(1)} collective-permute-done((bf16[16,5120]{1,0:T(8,128)(2,1)S(1)}, bf16[16,5120]{1,0:T(8,128)(2,1)S(1)}, u32[]{:S(2)}, u32[]{:S(2)}) %collective-permute-start.1) | collective-permute-done | bytes 163872 | tf_op jit(solution)/shard_map/ppermute | solution.py:18
  124.0 7.4 %collective-permute-done.2 = bf16[16,5120]{1,0:T(8,128)(2,1)S(1)} collective-permute-done((bf16[16,5120]{1,0:T(8,128)(2,1)S(1)}, bf16[16,5120]{1,0:T(8,128)(2,1)S(1)}, u32[]{:S(2)}, u32[]{:S(2)}) %collective-permute-start.2) | collective-permute-done | bytes 163872 | tf_op jit(solution)/shard_map/ppermute | solution.py:18
  131.4 7.4 %collective-permute-done.3 = bf16[16,5120]{1,0:T(8,128)(2,1)S(1)} collective-permute-done((bf16[16,5120]{1,0:T(8,128)(2,1)S(1)}, bf16[16,5120]{1,0:T(8,128)(2,1)S(1)}, u32[]{:S(2)}, u32[]{:S(2)}) %collective-permute-start.3) | collective-permute-done | bytes 163872 | tf_op jit(solution)/shard_map/ppermute | solution.py:18
  138.9 7.4 %collective-permute-done.4 = bf16[16,5120]{1,0:T(8,128)(2,1)S(1)} collective-permute-done((bf16[16,5120]{1,0:T(8,128)(2,1)S(1)}, bf16[16,5120]{1,0:T(8,128)(2,1)S(1)}, u32[]{:S(2)}, u32[]{:S(2)}) %collective-permute-start.4) | collective-permute-done | bytes 163872 | tf_op jit(solution)/shard_map/ppermute | solution.py:18
  146.3 7.4 %collective-permute-done.5 = bf16[16,5120]{1,0:T(8,128)(2,1)S(1)} collective-permute-done((bf16[16,5120]{1,0:T(8,128)(2,1)S(1)}, bf16[16,5120]{1,0:T(8,128)(2,1)S(1)}, u32[]{:S(2)}, u32[]{:S(2)}) %collective-permute-start.5) | collective-permute-done | bytes 163872 | tf_op jit(solution)/shard_map/ppermute | solution.py:18
  153.8 7.4 %collective-permute-done.6 = bf16[16,5120]{1,0:T(8,128)(2,1)S(1)} collective-permute-done((bf16[16,5120]{1,0:T(8,128)(2,1)S(1)}, bf16[16,5120]{1,0:T(8,128)(2,1)S(1)}, u32[]{:S(2)}, u32[]{:S(2)}) %collective-permute-start.6) | collective-permute-done | bytes 163872 | tf_op jit(solution)/shard_map/ppermute | solution.py:18
  161.2 7.4 %collective-permute-done.7 = bf16[16,5120]{1,0:T(8,128)(2,1)S(1)} collective-permute-done((bf16[16,5120]{1,0:T(8,128)(2,1)S(1)}, bf16[16,5120]{1,0:T(8,128)(2,1)S(1)}, u32[]{:S(2)}, u32[]{:S(2)}) %collective-permute-start.7) | collective-permute-done | bytes 163872 | tf_op jit(solution)/shard_map/ppermute | solution.py:18
  168.6 7.4 %collective-permute-done.8 = bf16[16,5120]{1,0:T(8,128)(2,1)S(1)} collective-permute-done((bf16[16,5120]{1,0:T(8,128)(2,1)S(1)}, bf16[16,5120]{1,0:T(8,128)(2,1)S(1)}, u32[]{:S(2)}, u32[]{:S(2)}) %collective-permute-start.8) | collective-permute-done | bytes 163872 | tf_op jit(solution)/shard_map/ppermute | solution.py:18
  176.1 7.4 %collective-permute-done.9 = bf16[16,5120]{1,0:T(8,128)(2,1)S(1)} collective-permute-done((bf16[16,5120]{1,0:T(8,128)(2,1)S(1)}, bf16[16,5120]{1,0:T(8,128)(2,1)S(1)}, u32[]{:S(2)}, u32[]{:S(2)}) %collective-permute-start.9) | collective-permute-done | bytes 163872 | tf_op jit(solution)/shard_map/ppermute | solution.py:18
  183.5 7.4 %collective-permute-done.10 = bf16[16,5120]{1,0:T(8,128)(2,1)S(1)} collective-permute-done((bf16[16,5120]{1,0:T(8,128)(2,1)S(1)}, bf16[16,5120]{1,0:T(8,128)(2,1)S(1)}, u32[]{:S(2)}, u32[]{:S(2)}) %collective-permute-start.10) | collective-permute-done | bytes 163872 | tf_op jit(solution)/shard_map/ppermute | solution.py:18
  191.0 7.4 %collective-permute-done.11 = bf16[16,5120]{1,0:T(8,128)(2,1)S(1)} collective-permute-done((bf16[16,5120]{1,0:T(8,128)(2,1)S(1)}, bf16[16,5120]{1,0:T(8,128)(2,1)S(1)}, u32[]{:S(2)}, u32[]{:S(2)}) %collective-permute-start.11) | collective-permute-done | bytes 163872 | tf_op jit(solution)/shard_map/ppermute | solution.py:18
  198.4 7.4 %collective-permute-done.12 = bf16[16,5120]{1,0:T(8,128)(2,1)S(1)} collective-permute-done((bf16[16,5120]{1,0:T(8,128)(2,1)S(1)}, bf16[16,5120]{1,0:T(8,128)(2,1)S(1)}, u32[]{:S(2)}, u32[]{:S(2)}) %collective-permute-start.12) | collective-permute-done | bytes 163872 | tf_op jit(solution)/shard_map/ppermute | solution.py:18
  205.9 7.4 %collective-permute-done.13 = bf16[16,5120]{1,0:T(8,128)(2,1)S(1)} collective-permute-done((bf16[16,5120]{1,0:T(8,128)(2,1)S(1)}, bf16[16,5120]{1,0:T(8,128)(2,1)S(1)}, u32[]{:S(2)}, u32[]{:S(2)}) %collective-permute-start.13) | collective-permute-done | bytes 163872 | tf_op jit(solution)/shard_map/ppermute | solution.py:18
  213.3 7.4 %collective-permute-done.14 = bf16[16,5120]{1,0:T(8,128)(2,1)S(1)} collective-permute-done((bf16[16,5120]{1,0:T(8,128)(2,1)S(1)}, bf16[16,5120]{1,0:T(8,128)(2,1)S(1)}, u32[]{:S(2)}, u32[]{:S(2)}) %collective-permute-start.14) | collective-permute-done | bytes 163872 | tf_op jit(solution)/shard_map/ppermute | solution.py:18
  230.9 0.8 constant_dynamic-update-slice_fusion.16
  242.6 32.2 %all-gather.8.cloned.1.call-done = bf16[5120,512]{1,0:T(8,128)(2,1)} async-done(((bf16[2560,512]{1,0:T(8,128)(2,1)}), bf16[5120,512]{1,0:T(8,128)(2,1)}) %all-gather.8.cloned.1.call-update) | async-done | bytes 5242896 | tf_op jit(solution)/shard_map/all_gather | solution.py:129
  274.8 4.8 fusion.5
  280.0 0.8 copy.48
  280.8 5.6 %all-to-all-start = ((bf16[16,16,512]{2,1,0:T(8,128)(2,1)}), bf16[16,16,512]{2,1,0:T(8,128)(2,1)S(1)}, u32[]{:S(2)}, u32[]{:S(2)}) async-start(bf16[16,16,512]{2,1,0:T(8,128)(2,1)} %copy.48), calls=%async_computation | async-start | bytes 524288 | tf_op jit(solution)/shard_map/all_to_all | solution.py:151
  289.8 1.3 fusion.45
  291.1 1.5 add_select_fusion.1
  292.6 3.9 all-to-all-done
  296.5 0.9 multiply_reduce_fusion
  298.1 28.0 %all_to_all.65 = bf16[128,2,4096]{2,0,1:T(8,128)(2,1)S(1)} all-to-all(bf16[128,2,4096]{2,0,1:T(8,128)(2,1)S(1)} %bitcast.111), channel_id=1, replica_groups=mesh['dp'=2,'ctx'=16] {'dp'}, dimensions={1} | all-to-all | bytes 4194304 | tf_op jit(solution)/shard_map/all_to_all | solution.py:170
  326.1 2.0 convolution_convert_fusion.5
  328.6 9.1 %reduce-scatter.3.cloned.1.call-done = bf16[128,512]{1,0:T(8,128)(2,1)} async-done(((bf16[256,512]{1,0:T(8,128)(2,1)}), bf16[128,512]{1,0:T(8,128)(2,1)}) %reduce-scatter.3.cloned.1.call-update) | async-done | bytes 131088 | tf_op jit(solution)/shard_map/reduce_scatter | solution.py:171
  337.7 1.0 reshape.495
  339.6 4.4 all_gather.15
  344.0 4.2 convolution_convert_fusion.2
  348.2 3.4 all-to-all-start.2
  352.2 4.7 all-to-all-done.2
  358.7 6.7 %copy.53 = bf16[1,16,8192]{1,0,2:T(2,128)(2,1)} copy(bf16[1,16,8192]{2,1,0:T(8,128)(2,1)S(1)} %select_convert_fusion) | data formatting | bytes 524288 | tf_op jit(solution)/shard_map/convert_element_type | solution.py:203
  365.9 45.2 %reduce.3 = bf16[8192,16]{1,0:T(8,128)(2,1)S(1)} reduce(bf16[8192,1,16]{2,1,0:T(2,128)(2,1)} %bitcast.108, bf16[]{:T(256)} %broadcast.491), dimensions={1}, to_apply=%bitcast.90.reduce_sub_computation | reduce | bytes 524290
  411.2 2.1 reshape.502
  413.3 15.4 %all_to_all.66 = bf16[16,2,4096]{2,1,0:T(2,128)(2,1)S(1)} all-to-all(bf16[16,2,4096]{2,1,0:T(2,128)(2,1)S(1)} %reshape.502), channel_id=1, replica_groups=mesh['dp'=2,'ctx'=16] {'ctx'}, dimensions={0} | all-to-all | bytes 524288 | tf_op jit(solution)/shard_map/all_to_all | solution.py:204
  428.8 7.6 %reshape.503 = bf16[8192,1,16]{2,1,0:T(2,128)(2,1)} reshape(bf16[16,2,4096]{2,1,0:T(2,128)(2,1)S(1)} %all_to_all.66) | data formatting | bytes 524288
  436.3 7.9 %copy.54 = bf16[1,16,8192]{2,1,0:T(8,128)(2,1)S(1)} copy(bf16[1,16,8192]{1,0,2:T(2,128)(2,1)} %bitcast.109) | data formatting | bytes 524288 | tf_op jit(solution)/shard_map/all_to_all | solution.py:204
  444.7 5.6 %convolution_convert_fusion.1 = bf16[5120,512]{1,0:T(8,128)(2,1)} fusion(bf16[256,512]{1,0:T(8,128)(2,1)S(1)} %bitcast.116, bf16[512,5120]{1,0:T(8,128)(2,1)} %constant_dynamic-update-slice_fusion, s32[]{:T(128)S(6)} %select_n.126), kind=kOutput, calls=%fused_computation.3 | convolution fusion | flops 1344798720 | bytes 8126468 | tf_op jit(solution)/shard_map/dot_general | solution.py:210
  451.3 62.3 %reduce-scatter.5.cloned.1.call-done = bf16[2560,512]{1,0:T(8,128)(2,1)} async-done(((bf16[5120,512]{1,0:T(8,128)(2,1)}), bf16[2560,512]{1,0:T(8,128)(2,1)}) %reduce-scatter.5.cloned.1.call-update) | async-done | bytes 2621456 | tf_op jit(solution)/shard_map/reduce_scatter | solution.py:209
  513.5 4.8 convert_element_type.196
  (118 shorter events, 33.0 us)
Async XLA Ops:
  7.2 69.9 %all-gather.4.cloned.1.call-start = ((), (), s32[]{:S(2)}) async-start(), calls=%async_computation.6 | async-start | bytes 7372800 | tf_op jit(solution)/shard_map/all_gather | solution.py:127
  7.9 98.7 %copy-start.1 = (bf16[1,64,1280]{2,1,0:T(8,128)(2,1)S(1)}, bf16[1,64,1280]{2,1,0:T(8,128)(2,1)}, u32[]{:S(2)}) copy-start(bf16[1,64,1280]{2,1,0:T(8,128)(2,1)} %param.11) | copy-start | bytes 491524
  7.9 98.7 %all-gather.6.cloned.1.call-start = ((), (), s32[]{:S(2)}) async-start(), calls=%async_computation.7 | async-start | bytes 2457600 | tf_op jit(solution)/shard_map/all_gather | solution.py:128
  8.7 266.2 %all-gather.8.cloned.1.call-start = ((), (), s32[]{:S(2)}) async-start(), calls=%async_computation.8 | async-start | bytes 7864320 | tf_op jit(solution)/shard_map/all_gather | solution.py:129
  80.6 132.7 %copy-start.5 = (s32[1,16]{1,0:T(1,128)S(1)}, s32[1,16]{1,0:T(1,128)}, u32[]{:S(2)}) copy-start(s32[1,16]{1,0:T(1,128)} %param.21) | copy-start | bytes 196
  109.1 7.5 %collective-permute-start = (bf16[16,5120]{1,0:T(8,128)(2,1)S(1)}, bf16[16,5120]{1,0:T(8,128)(2,1)S(1)}, u32[]{:S(2)}, u32[]{:S(2)}) collective-permute-start(bf16[16,5120]{1,0:T(8,128)(2,1)S(1)} %broadcast_select_fusion), channel_id=1, source_target_pairs={{0,1},{1,2},{2,3},{3,4},{4,5},{5,6},{6,7},{7,8},{8,9},{9,10},{10,1... | collective-permute-start | bytes 491528 | tf_op jit(solution)/shard_map/ppermute | solution.py:18
  116.6 7.4 %collective-permute-start.1 = (bf16[16,5120]{1,0:T(8,128)(2,1)S(1)}, bf16[16,5120]{1,0:T(8,128)(2,1)S(1)}, u32[]{:S(2)}, u32[]{:S(2)}) collective-permute-start(bf16[16,5120]{1,0:T(8,128)(2,1)S(1)} %collective-permute-done), channel_id=1, source_target_pairs={{0,1},{1,2},{2,3},{3,4},{4,5},{5,6},{6,7},{7,8},{8,9},{9,10},{10,1... | collective-permute-start | bytes 491528 | tf_op jit(solution)/shard_map/ppermute | solution.py:18
  124.0 7.4 %collective-permute-start.2 = (bf16[16,5120]{1,0:T(8,128)(2,1)S(1)}, bf16[16,5120]{1,0:T(8,128)(2,1)S(1)}, u32[]{:S(2)}, u32[]{:S(2)}) collective-permute-start(bf16[16,5120]{1,0:T(8,128)(2,1)S(1)} %collective-permute-done.1), channel_id=1, source_target_pairs={{0,1},{1,2},{2,3},{3,4},{4,5},{5,6},{6,7},{7,8},{8,9},{9,10},{10,1... | collective-permute-start | bytes 491528 | tf_op jit(solution)/shard_map/ppermute | solution.py:18
  131.4 7.4 %collective-permute-start.3 = (bf16[16,5120]{1,0:T(8,128)(2,1)S(1)}, bf16[16,5120]{1,0:T(8,128)(2,1)S(1)}, u32[]{:S(2)}, u32[]{:S(2)}) collective-permute-start(bf16[16,5120]{1,0:T(8,128)(2,1)S(1)} %collective-permute-done.2), channel_id=1, source_target_pairs={{0,1},{1,2},{2,3},{3,4},{4,5},{5,6},{6,7},{7,8},{8,9},{9,10},{10,1... | collective-permute-start | bytes 491528 | tf_op jit(solution)/shard_map/ppermute | solution.py:18
  138.9 7.4 %collective-permute-start.4 = (bf16[16,5120]{1,0:T(8,128)(2,1)S(1)}, bf16[16,5120]{1,0:T(8,128)(2,1)S(1)}, u32[]{:S(2)}, u32[]{:S(2)}) collective-permute-start(bf16[16,5120]{1,0:T(8,128)(2,1)S(1)} %collective-permute-done.3), channel_id=1, source_target_pairs={{0,1},{1,2},{2,3},{3,4},{4,5},{5,6},{6,7},{7,8},{8,9},{9,10},{10,1... | collective-permute-start | bytes 491528 | tf_op jit(solution)/shard_map/ppermute | solution.py:18
  146.3 7.4 %collective-permute-start.5 = (bf16[16,5120]{1,0:T(8,128)(2,1)S(1)}, bf16[16,5120]{1,0:T(8,128)(2,1)S(1)}, u32[]{:S(2)}, u32[]{:S(2)}) collective-permute-start(bf16[16,5120]{1,0:T(8,128)(2,1)S(1)} %collective-permute-done.4), channel_id=1, source_target_pairs={{0,1},{1,2},{2,3},{3,4},{4,5},{5,6},{6,7},{7,8},{8,9},{9,10},{10,1... | collective-permute-start | bytes 491528 | tf_op jit(solution)/shard_map/ppermute | solution.py:18
  153.8 7.4 %collective-permute-start.6 = (bf16[16,5120]{1,0:T(8,128)(2,1)S(1)}, bf16[16,5120]{1,0:T(8,128)(2,1)S(1)}, u32[]{:S(2)}, u32[]{:S(2)}) collective-permute-start(bf16[16,5120]{1,0:T(8,128)(2,1)S(1)} %collective-permute-done.5), channel_id=1, source_target_pairs={{0,1},{1,2},{2,3},{3,4},{4,5},{5,6},{6,7},{7,8},{8,9},{9,10},{10,1... | collective-permute-start | bytes 491528 | tf_op jit(solution)/shard_map/ppermute | solution.py:18
  161.2 7.4 %collective-permute-start.7 = (bf16[16,5120]{1,0:T(8,128)(2,1)S(1)}, bf16[16,5120]{1,0:T(8,128)(2,1)S(1)}, u32[]{:S(2)}, u32[]{:S(2)}) collective-permute-start(bf16[16,5120]{1,0:T(8,128)(2,1)S(1)} %collective-permute-done.6), channel_id=1, source_target_pairs={{0,1},{1,2},{2,3},{3,4},{4,5},{5,6},{6,7},{7,8},{8,9},{9,10},{10,1... | collective-permute-start | bytes 491528 | tf_op jit(solution)/shard_map/ppermute | solution.py:18
  168.6 7.4 %collective-permute-start.8 = (bf16[16,5120]{1,0:T(8,128)(2,1)S(1)}, bf16[16,5120]{1,0:T(8,128)(2,1)S(1)}, u32[]{:S(2)}, u32[]{:S(2)}) collective-permute-start(bf16[16,5120]{1,0:T(8,128)(2,1)S(1)} %collective-permute-done.7), channel_id=1, source_target_pairs={{0,1},{1,2},{2,3},{3,4},{4,5},{5,6},{6,7},{7,8},{8,9},{9,10},{10,1... | collective-permute-start | bytes 491528 | tf_op jit(solution)/shard_map/ppermute | solution.py:18
  176.1 7.4 %collective-permute-start.9 = (bf16[16,5120]{1,0:T(8,128)(2,1)S(1)}, bf16[16,5120]{1,0:T(8,128)(2,1)S(1)}, u32[]{:S(2)}, u32[]{:S(2)}) collective-permute-start(bf16[16,5120]{1,0:T(8,128)(2,1)S(1)} %collective-permute-done.8), channel_id=1, source_target_pairs={{0,1},{1,2},{2,3},{3,4},{4,5},{5,6},{6,7},{7,8},{8,9},{9,10},{10,1... | collective-permute-start | bytes 491528 | tf_op jit(solution)/shard_map/ppermute | solution.py:18
  183.5 7.4 %collective-permute-start.10 = (bf16[16,5120]{1,0:T(8,128)(2,1)S(1)}, bf16[16,5120]{1,0:T(8,128)(2,1)S(1)}, u32[]{:S(2)}, u32[]{:S(2)}) collective-permute-start(bf16[16,5120]{1,0:T(8,128)(2,1)S(1)} %collective-permute-done.9), channel_id=1, source_target_pairs={{0,1},{1,2},{2,3},{3,4},{4,5},{5,6},{6,7},{7,8},{8,9},{9,10},{10,1... | collective-permute-start | bytes 491528 | tf_op jit(solution)/shard_map/ppermute | solution.py:18
  191.0 7.4 %collective-permute-start.11 = (bf16[16,5120]{1,0:T(8,128)(2,1)S(1)}, bf16[16,5120]{1,0:T(8,128)(2,1)S(1)}, u32[]{:S(2)}, u32[]{:S(2)}) collective-permute-start(bf16[16,5120]{1,0:T(8,128)(2,1)S(1)} %collective-permute-done.10), channel_id=1, source_target_pairs={{0,1},{1,2},{2,3},{3,4},{4,5},{5,6},{6,7},{7,8},{8,9},{9,10},{10,1... | collective-permute-start | bytes 491528 | tf_op jit(solution)/shard_map/ppermute | solution.py:18
  198.4 7.4 %collective-permute-start.12 = (bf16[16,5120]{1,0:T(8,128)(2,1)S(1)}, bf16[16,5120]{1,0:T(8,128)(2,1)S(1)}, u32[]{:S(2)}, u32[]{:S(2)}) collective-permute-start(bf16[16,5120]{1,0:T(8,128)(2,1)S(1)} %collective-permute-done.11), channel_id=1, source_target_pairs={{0,1},{1,2},{2,3},{3,4},{4,5},{5,6},{6,7},{7,8},{8,9},{9,10},{10,1... | collective-permute-start | bytes 491528 | tf_op jit(solution)/shard_map/ppermute | solution.py:18
  205.8 7.4 %collective-permute-start.13 = (bf16[16,5120]{1,0:T(8,128)(2,1)S(1)}, bf16[16,5120]{1,0:T(8,128)(2,1)S(1)}, u32[]{:S(2)}, u32[]{:S(2)}) collective-permute-start(bf16[16,5120]{1,0:T(8,128)(2,1)S(1)} %collective-permute-done.12), channel_id=1, source_target_pairs={{0,1},{1,2},{2,3},{3,4},{4,5},{5,6},{6,7},{7,8},{8,9},{9,10},{10,1... | collective-permute-start | bytes 491528 | tf_op jit(solution)/shard_map/ppermute | solution.py:18
  213.3 7.4 %collective-permute-start.14 = (bf16[16,5120]{1,0:T(8,128)(2,1)S(1)}, bf16[16,5120]{1,0:T(8,128)(2,1)S(1)}, u32[]{:S(2)}, u32[]{:S(2)}) collective-permute-start(bf16[16,5120]{1,0:T(8,128)(2,1)S(1)} %collective-permute-done.13), channel_id=1, source_target_pairs={{0,1},{1,2},{2,3},{3,4},{4,5},{5,6},{6,7},{7,8},{8,9},{9,10},{10,1... | collective-permute-start | bytes 491528 | tf_op jit(solution)/shard_map/ppermute | solution.py:18
  242.6 53.9 %copy-start.2 = (bf16[1,128,8192]{2,1,0:T(8,128)(2,1)S(1)}, bf16[1,128,8192]{2,1,0:T(8,128)(2,1)}, u32[]{:S(2)}) copy-start(bf16[1,128,8192]{2,1,0:T(8,128)(2,1)} %param.16) | copy-start | bytes 6291460
  279.6 17.8 %copy-start.3 = (f32[8192]{0:T(1024)S(1)}, f32[8192]{0:T(1024)}, u32[]{:S(2)}) copy-start(f32[8192]{0:T(1024)} %param.17) | copy-start | bytes 98308
  280.8 15.6 %all-to-all-start = ((bf16[16,16,512]{2,1,0:T(8,128)(2,1)}), bf16[16,16,512]{2,1,0:T(8,128)(2,1)S(1)}, u32[]{:S(2)}, u32[]{:S(2)}) async-start(bf16[16,16,512]{2,1,0:T(8,128)(2,1)} %copy.48), calls=%async_computation | async-start | bytes 524288 | tf_op jit(solution)/shard_map/all_to_all | solution.py:151
  286.5 51.2 %reduce-scatter.3.cloned.1.call-start = ((), (), s32[]{:S(2)}) async-start(), calls=%async_computation.9 | async-start | bytes 393216 | tf_op jit(solution)/shard_map/reduce_scatter | solution.py:171
  297.9 28.2 %copy-start = (bf16[4096,512]{1,0:T(8,128)(2,1)S(1)}, bf16[4096,512]{1,0:T(8,128)(2,1)}, u32[]{:S(2)}) copy-start(bf16[4096,512]{1,0:T(8,128)(2,1)} %param.18) | copy-start | bytes 12582916
  298.1 30.1 %copy-start.4 = (bf16[1,128,512]{2,1,0:T(8,128)(2,1)S(1)}, bf16[1,128,512]{2,1,0:T(8,128)(2,1)}, u32[]{:S(2)}) copy-start(bf16[1,128,512]{2,1,0:T(8,128)(2,1)} %param.19) | copy-start | bytes 393220
  348.2 8.6 %all-to-all-start.2 = ((bf16[2,16,4096]{2,1,0:T(8,128)(2,1)}), bf16[2,16,4096]{2,1,0:T(8,128)(2,1)S(1)}, u32[]{:S(2)}, u32[]{:S(2)}) async-start(bf16[2,16,4096]{2,1,0:T(8,128)(2,1)} %bitcast.17), calls=%async_computation.3 | async-start | bytes 524288 | tf_op jit(solution)/shard_map/all_to_all | solution.py:199
  351.7 161.9 %reduce-scatter.5.cloned.1.call-start = ((), (), s32[]{:S(2)}) async-start(), calls=%async_computation.10 | async-start | bytes 7864320 | tf_op jit(solution)/shard_map/reduce_scatter | solution.py:209
Sparse Core Ops, SparseCore 0:
  9.5 67.5 all-gather.3
  78.6 27.9 all-gather.5
  206.0 68.7 all-gather.7
  328.2 9.3 reduce-scatter.2
  450.5 63.0 reduce-scatter.4
